TPU v7x, 512 devices: a whole 4x4x16 slice. The times are simulated.
512 devices in a mesh: node: 32 (over y, x, core), freq: 16 (over z).
Axes of the slice: x: 4, y: 4, z: 16, core: 2. Of those that a mesh axis runs over, the one named last changes fastest.
Arguments:
- density: float32 [256, 16, 8192], P('freq', None, 'node'), may hold values from -6 to 6
- coords: float32 [3, 8192], P(None, 'node'), may hold values from -12 to 12
- weights: float32 [8192], P('node'), may hold values from 0.1 to 1
- neighbours: int32 [64, 4], P('node'), may hold values from 0 to 63, as said below
- counts: int32 [64], P('node'), may hold values from 1 to 4, as said below
Outputs:
- field: float32 [256, 16, 8192], P('freq', None, 'node')
Inputs may be any that keep to these rules, and one draw needn't show every extreme that they name: `neighbours`: row p starts with p itself, then lists distinct patches that lie within 2 places of p in the cyclic order of patches; only the first counts[p] entries of a row are used, the rest are valid patch numbers. `counts`: some patch uses all 4 entries.
All inputs are finite; a program needn't handle non-finite values.
Results may differ from a plain program's by a relative error of at most 0.0003.
Values sent between devices are 32-bit elements; how exact they have to be, the bound alone decides.
A program may use at most 64 MiB of HBM per device.

v0:
```python
import jax
import jax.numpy as jnp
from jax import lax
from jax.sharding import PartitionSpec as P

STEPS = 256
PATCH = 128
PATCH_DEV = 2
NEAR_MOST = 4


decay_ratio = 0.1
time_step = 1.0
smoothing = 0.5
highest = lax.Precision.HIGHEST


def padded_2(cells, sides, width):
    for axis, dim in sides:
        count = lax.axis_size(axis)
        head = lax.slice_in_dim(cells, 0, width, axis=dim)
        tail = lax.slice_in_dim(cells, cells.shape[dim] - width, cells.shape[dim], axis=dim)
        cells = jnp.concatenate(
            [
                lax.ppermute(tail, axis, [(i, (i + 1) % count) for i in range(count)]),
                cells,
                lax.ppermute(head, axis, [((i + 1) % count, i) for i in range(count)]),
            ],
            axis=dim,
        )
    return cells


def fourier_tables(freq_count):
    freq_index = jnp.arange(freq_count, dtype=jnp.int32)
    time_index = jnp.arange(STEPS, dtype=jnp.int32)
    phase_index = (2 * freq_index[:, None] + 1) * time_index[None, :] % (2 * STEPS)
    phase_angle = phase_index.astype(jnp.float32) * (jnp.pi / STEPS)
    return (jnp.cos(phase_angle), jnp.sin(phase_angle))


def laplace_values(freq_index):
    phase_angle = (2 * freq_index + 1).astype(jnp.float32) * (jnp.pi / STEPS)
    radius = decay_ratio ** (1.0 / STEPS)
    offset_real = 1.0 - radius * jnp.cos(phase_angle)
    offset_imag = -radius * jnp.sin(phase_angle)
    delta_real = offset_real + 0.5 * (offset_real * offset_real - offset_imag * offset_imag)
    delta_imag = offset_imag + offset_real * offset_imag
    return (delta_real / time_step, delta_imag / time_step)


def time_weights(time_index, sign):
    radius = decay_ratio ** (1.0 / STEPS)
    return jnp.power(jnp.float32(radius), sign * time_index.astype(jnp.float32))


def kernel_terms(distance, static_part, value_real, value_imag):
    decaying = jnp.exp(-value_real * distance) * static_part
    return (decaying * jnp.cos(value_imag * distance), -decaying * jnp.sin(value_imag * distance))


def body(density, coords, weights, neighbours, counts):
    local_times = density.shape[0]
    fields_here = density.shape[1]
    width = density.shape[2]
    freq_parts = lax.axis_size("freq")
    node_parts = lax.axis_size("node")
    spectrum_count = STEPS // 2
    factor = 2.0
    cosine, sine = fourier_tables(spectrum_count)
    own_times = lax.axis_index("freq") * local_times + jnp.arange(local_times, dtype=jnp.int32)
    scaled = density * time_weights(own_times, 1.0)[:, None, None]
    gathered_block = lax.all_to_all(scaled, "freq", split_axis=2, concat_axis=0, tiled=True)
    item_count = gathered_block.shape[1]
    column_count = gathered_block.shape[2]
    flattened = gathered_block.reshape(STEPS, item_count * column_count)
    part_real = jnp.dot(cosine, flattened, precision=highest, preferred_element_type=jnp.float32)
    part_imag = jnp.dot(sine, flattened, precision=highest, preferred_element_type=jnp.float32)
    spectrum = jnp.stack([part_real, part_imag], axis=1).reshape(
        spectrum_count, 2, item_count, column_count
    )
    own_spectrum = lax.all_to_all(spectrum, "freq", split_axis=0, concat_axis=3, tiled=True)
    local_freqs = spectrum_count // freq_parts
    rows_spec = local_freqs * 2 * fields_here
    packed = jnp.concatenate(
        [own_spectrum.reshape(rows_spec, width), coords, weights[None, :]], axis=0
    )
    padded = padded_2(packed, (("node", 1),), width)
    total_patches = PATCH_DEV * node_parts
    first_patch = (lax.axis_index("node") - 1) * PATCH_DEV
    local_slots = (neighbours - first_patch) % total_patches
    columns = (
        local_slots[:, :, None] * PATCH + jnp.arange(PATCH, dtype=jnp.int32)[None, None, :]
    ).reshape(PATCH_DEV, NEAR_MOST * PATCH)
    geometry = padded[rows_spec:]
    other_coords = geometry[:3][:, columns]
    live_slots = (jnp.arange(NEAR_MOST, dtype=jnp.int32)[None, :] < counts[:, None]).astype(
        jnp.float32
    )
    node_scale = geometry[3][columns] * jnp.repeat(live_slots, PATCH, axis=1)
    own_coords = coords.reshape(3, PATCH_DEV, PATCH)
    separation = own_coords[:, :, :, None] - other_coords[:, :, None, :]
    distance = jnp.sqrt(jnp.sum(separation * separation, axis=0) + smoothing * smoothing)
    static_part = node_scale[:, None, :] / (4.0 * jnp.pi * distance)
    spectra = padded[:rows_spec].reshape(local_freqs, 2, fields_here, 3 * width)
    freq_index = lax.axis_index("freq") * local_freqs + jnp.arange(local_freqs, dtype=jnp.int32)
    laplace_real, laplace_imag = laplace_values(freq_index)

    def one_freq(arguments):
        value_real, value_imag, freq_block = arguments
        picked = freq_block[:, :, columns]
        kern_real, kern_imag = kernel_terms(distance, static_part, value_real, value_imag)
        out_real = jnp.einsum("pij,rpj->rpi", kern_real, picked[0], precision=highest) - jnp.einsum(
            "pij,rpj->rpi", kern_imag, picked[1], precision=highest
        )
        out_imag = jnp.einsum("pij,rpj->rpi", kern_real, picked[1], precision=highest) + jnp.einsum(
            "pij,rpj->rpi", kern_imag, picked[0], precision=highest
        )
        return jnp.stack([out_real, out_imag]).reshape(2, fields_here, width)

    near_field = lax.map(one_freq, (laplace_real, laplace_imag, spectra))
    gathered_block = lax.all_to_all(near_field, "freq", split_axis=3, concat_axis=0, tiled=True)
    item_count = gathered_block.shape[2]
    column_count = gathered_block.shape[3]
    block_real = gathered_block[:, 0].reshape(spectrum_count, item_count * column_count)
    block_imag = gathered_block[:, 1].reshape(spectrum_count, item_count * column_count)
    summed = jnp.dot(
        cosine.T, block_real, precision=highest, preferred_element_type=jnp.float32
    ) + jnp.dot(sine.T, block_imag, precision=highest, preferred_element_type=jnp.float32)
    all_times = jnp.arange(STEPS, dtype=jnp.int32)
    summed = summed * (factor / STEPS) * time_weights(all_times, -1.0)[:, None]
    time_domain = summed.reshape(STEPS, item_count, column_count)
    return lax.all_to_all(time_domain, "freq", split_axis=0, concat_axis=2, tiled=True)


def solution(mesh):
    placed = (P("freq", None, "node"), P(None, "node"), P("node"), P("node", None), P("node"))
    return jax.shard_map(
        body, mesh=mesh, in_specs=placed, out_specs=P("freq", None, "node"), check_vma=False
    )
```

profile of v0, /device:TPU:24, one launch (start us, length us, event | category | flops | bytes accessed | tf_op | source)
XLA Modules:
  0.0 347.0 jit_solution(16932057424329263771)
XLA Ops:
  3.8 15.2 %all-to-all-start = ((f32[16,1,4096]{2,1,0:T(1,128)}), f32[16,1,4096]{2,1,0:T(1,128)S(1)}, u32[]{:S(2)}, u32[]{:S(2)}) async-start(f32[16,1,4096]{2,1,0:T(1,128)} %reshape.176), calls=%async_computation | async-start | bytes 524288 | tf_op jit(solution)/shard_map/all_to_all | solution.py:73
  19.3 18.1 %all-to-all-done = f32[16,1,4096]{2,1,0:T(1,128)S(1)} async-done(((f32[16,1,4096]{2,1,0:T(1,128)}), f32[16,1,4096]{2,1,0:T(1,128)S(1)}, u32[]{:S(2)}, u32[]{:S(2)}) %all-to-all-start) | async-done | bytes 262176 | tf_op jit(solution)/shard_map/all_to_all | solution.py:73
  50.2 5.8 %all-to-all-start.1 = ((f32[16,1,4096]{2,1,0:T(1,128)}), f32[16,1,4096]{2,1,0:T(1,128)S(1)}, u32[]{:S(2)}, u32[]{:S(2)}) async-start(f32[16,1,4096]{2,1,0:T(1,128)} %reshape.178), calls=%async_computation.1 | async-start | bytes 524288 | tf_op jit(solution)/shard_map/all_to_all | solution.py:82
  56.3 18.2 %all-to-all-done.1 = f32[16,1,4096]{2,1,0:T(1,128)S(1)} async-done(((f32[16,1,4096]{2,1,0:T(1,128)}), f32[16,1,4096]{2,1,0:T(1,128)S(1)}, u32[]{:S(2)}, u32[]{:S(2)}) %all-to-all-start.1) | async-done | bytes 262176 | tf_op jit(solution)/shard_map/all_to_all | solution.py:82
  78.9 4.2 %reshape.137 = f32[256,256]{0,1:T(8,128)S(1)} reshape(f32[8,2,16,16,16]{2,1,0,4,3:T(2,128)} %copy.75) | data formatting | bytes 524288 | tf_op jit(solution)/shard_map/reshape | solution.py:86
  85.2 5.8 %collective-permute-start.1 = (f32[260,256]{0,1:T(8,128)S(1)}, f32[260,256]{0,1:T(8,128)S(1)}, u32[]{:S(2)}, u32[]{:S(2)}) collective-permute-start(f32[260,256]{0,1:T(8,128)S(1)} %pad_maximum_fusion.1), channel_id=1, source_target_pairs={{16,0},{32,16},{48,32},{64,48},{80,64},{96,80},{112,96},{128,112},... | collective-permute-start | bytes 798728 | tf_op jit(solution)/shard_map/ppermute | solution.py:27
  91.1 3.4 collective-permute-done
  99.7 4.5 %gather_fusion.2 = f32[1024]{0:T(1024)S(1)} fusion(f32[768]{0:T(1024)S(1)} %slice_reduce_fusion, s32[1024]{0:T(1024)S(1)} %broadcast_clamp_fusion.1), kind=kCustom, calls=%fused_computation.2 | custom fusion | bytes 12288 | tf_op jit(solution)/shard_map/gather | solution.py:100
  105.9 165.3 %while.11 = (s32[]{:T(128)}, f32[8,2,16,256]{3,2,1,0:T(8,128)S(1)}, f32[8,2,16,768]{3,2,1,0:T(8,128)}, f32[8]{0:T(128)S(1)}, f32[2,128,512]{2,1,0:T(8,128)S(1)},...) while((s32[]{:T(128)}, f32[8,2,16,256]{3,2,1,0:T(8,128)S(1)}, ...), condition=%wide.region_2.3_spmd.clone, body=%wide.region_1.2_spmd.clone.sunk | while | flops 103044096 | bytes 5703885 | solution.py:121
  107.3 3.5 %gather_fusion = f32[1024,2,16]{2,1,0:T(2,128)S(1)} fusion(f32[2,16,768]{1,0,2:T(2,128)S(1)} %bitcast.130, s32[1024]{0:T(1024)S(1)} %broadcast_clamp_fusion.3), kind=kCustom, calls=%fused_computation.clone.clone.1 | custom fusion | bytes 266240 | tf_op jit(solution)/shard_map/while/body/eval_jaxpr/gather | solution.py:111
  116.4 3.4 fusion.57
  123.1 3.4 fusion.55
  128.0 3.5 %gather_fusion = f32[1024,2,16]{2,1,0:T(2,128)S(1)} fusion(f32[2,16,768]{1,0,2:T(2,128)S(1)} %bitcast.130, s32[1024]{0:T(1024)S(1)} %broadcast_clamp_fusion.3), kind=kCustom, calls=%fused_computation.clone.clone.1 | custom fusion | bytes 266240 | tf_op jit(solution)/shard_map/while/body/eval_jaxpr/gather | solution.py:111
  137.0 3.4 fusion.57
  143.8 3.4 fusion.55
  148.7 3.5 %gather_fusion = f32[1024,2,16]{2,1,0:T(2,128)S(1)} fusion(f32[2,16,768]{1,0,2:T(2,128)S(1)} %bitcast.130, s32[1024]{0:T(1024)S(1)} %broadcast_clamp_fusion.3), kind=kCustom, calls=%fused_computation.clone.clone.1 | custom fusion | bytes 266240 | tf_op jit(solution)/shard_map/while/body/eval_jaxpr/gather | solution.py:111
  157.7 3.4 fusion.57
  164.4 3.4 fusion.55
  169.3 3.5 %gather_fusion = f32[1024,2,16]{2,1,0:T(2,128)S(1)} fusion(f32[2,16,768]{1,0,2:T(2,128)S(1)} %bitcast.130, s32[1024]{0:T(1024)S(1)} %broadcast_clamp_fusion.3), kind=kCustom, calls=%fused_computation.clone.clone.1 | custom fusion | bytes 266240 | tf_op jit(solution)/shard_map/while/body/eval_jaxpr/gather | solution.py:111
  178.4 3.4 fusion.57
  185.1 3.4 fusion.55
  190.0 3.5 %gather_fusion = f32[1024,2,16]{2,1,0:T(2,128)S(1)} fusion(f32[2,16,768]{1,0,2:T(2,128)S(1)} %bitcast.130, s32[1024]{0:T(1024)S(1)} %broadcast_clamp_fusion.3), kind=kCustom, calls=%fused_computation.clone.clone.1 | custom fusion | bytes 266240 | tf_op jit(solution)/shard_map/while/body/eval_jaxpr/gather | solution.py:111
  210.6 3.5 %gather_fusion = f32[1024,2,16]{2,1,0:T(2,128)S(1)} fusion(f32[2,16,768]{1,0,2:T(2,128)S(1)} %bitcast.130, s32[1024]{0:T(1024)S(1)} %broadcast_clamp_fusion.3), kind=kCustom, calls=%fused_computation.clone.clone.1 | custom fusion | bytes 266240 | tf_op jit(solution)/shard_map/while/body/eval_jaxpr/gather | solution.py:111
  219.7 3.4 fusion.57
  226.4 3.4 fusion.55
  231.3 3.5 %gather_fusion = f32[1024,2,16]{2,1,0:T(2,128)S(1)} fusion(f32[2,16,768]{1,0,2:T(2,128)S(1)} %bitcast.130, s32[1024]{0:T(1024)S(1)} %broadcast_clamp_fusion.3), kind=kCustom, calls=%fused_computation.clone.clone.1 | custom fusion | bytes 266240 | tf_op jit(solution)/shard_map/while/body/eval_jaxpr/gather | solution.py:111
  252.0 3.5 %gather_fusion = f32[1024,2,16]{2,1,0:T(2,128)S(1)} fusion(f32[2,16,768]{1,0,2:T(2,128)S(1)} %bitcast.130, s32[1024]{0:T(1024)S(1)} %broadcast_clamp_fusion.3), kind=kCustom, calls=%fused_computation.clone.clone.1 | custom fusion | bytes 266240 | tf_op jit(solution)/shard_map/while/body/eval_jaxpr/gather | solution.py:111
  272.7 3.6 %reshape.180 = f32[16,1,4096]{2,1,0:T(1,128)} reshape(f32[256,8,2,16]{3,2,1,0:T(2,128)S(1)} %bitcast.132) | data formatting | bytes 524288
  276.3 5.6 %all-to-all-start.2 = ((f32[16,1,4096]{2,1,0:T(1,128)}), f32[16,1,4096]{2,1,0:T(1,128)S(1)}, u32[]{:S(2)}, u32[]{:S(2)}) async-start(f32[16,1,4096]{2,1,0:T(1,128)} %reshape.180), calls=%async_computation.2 | async-start | bytes 524288 | tf_op jit(solution)/shard_map/all_to_all | solution.py:122
  281.8 18.4 %all-to-all-done.2 = f32[16,1,4096]{2,1,0:T(1,128)S(1)} async-done(((f32[16,1,4096]{2,1,0:T(1,128)}), f32[16,1,4096]{2,1,0:T(1,128)S(1)}, u32[]{:S(2)}, u32[]{:S(2)}) %all-to-all-start.2) | async-done | bytes 262176 | tf_op jit(solution)/shard_map/all_to_all | solution.py:122
  301.5 4.1 %reshape.181 = f32[256,8,2,16]{3,2,1,0:T(2,128)} reshape(f32[16,4096]{1,0:T(8,128)S(1)} %reduce.4) | data formatting | bytes 524288
  315.6 23.9 %all_to_all.66 = f32[16,1,4096]{2,1,0:T(1,128)S(1)} all-to-all(f32[16,1,4096]{2,1,0:T(1,128)S(1)} %reshape.182), channel_id=1, replica_groups=mesh['node'=32,'freq'=16] {'freq'}, dimensions={0} | all-to-all | bytes 524288 | tf_op jit(solution)/shard_map/all_to_all | solution.py:133
  (203 shorter events, 148.6 us)
Async XLA Ops:
  2.3 16.7 %copy-start = (f32[3,256]{1,0:T(4,128)S(1)}, f32[3,256]{1,0:T(4,128)}, u32[]{:S(2)}) copy-start(f32[3,256]{1,0:T(4,128)} %param.8) | copy-start | bytes 9220
  2.4 16.8 %copy-start.1 = (f32[256]{0:T(256)S(1)}, f32[256]{0:T(256)}, u32[]{:S(2)}) copy-start(f32[256]{0:T(256)} %param.9) | copy-start | bytes 3076
  3.8 33.6 %all-to-all-start = ((f32[16,1,4096]{2,1,0:T(1,128)}), f32[16,1,4096]{2,1,0:T(1,128)S(1)}, u32[]{:S(2)}, u32[]{:S(2)}) async-start(f32[16,1,4096]{2,1,0:T(1,128)} %reshape.176), calls=%async_computation | async-start | bytes 524288 | tf_op jit(solution)/shard_map/all_to_all | solution.py:73
  48.7 7.3 %copy-start.2 = (s32[2,4]{1,0:T(2,128)S(1)}, s32[2,4]{1,0:T(2,128)}, u32[]{:S(2)}) copy-start(s32[2,4]{1,0:T(2,128)} %param.10) | copy-start | bytes 100
  48.7 7.4 %copy-start.3 = (s32[2]{0:T(128)S(1)}, s32[2]{0:T(128)}, u32[]{:S(2)}) copy-start(s32[2]{0:T(128)} %param.11) | copy-start | bytes 28
  50.2 24.3 %all-to-all-start.1 = ((f32[16,1,4096]{2,1,0:T(1,128)}), f32[16,1,4096]{2,1,0:T(1,128)S(1)}, u32[]{:S(2)}, u32[]{:S(2)}) async-start(f32[16,1,4096]{2,1,0:T(1,128)} %reshape.178), calls=%async_computation.1 | async-start | bytes 524288 | tf_op jit(solution)/shard_map/all_to_all | solution.py:82
  83.3 11.2 %collective-permute-start = (f32[260,256]{0,1:T(8,128)S(1)}, f32[260,256]{0,1:T(8,128)S(1)}, u32[]{:S(2)}, u32[]{:S(2)}) collective-permute-start(f32[260,256]{0,1:T(8,128)S(1)} %pad_maximum_fusion.1), channel_id=1, source_target_pairs={{0,16},{16,32},{32,48},{48,64},{64,80},{80,96},{96,112},{112,128},... | collective-permute-start | bytes 798728 | tf_op jit(solution)/shard_map/ppermute | solution.py:25
  85.2 11.0 %collective-permute-start.1 = (f32[260,256]{0,1:T(8,128)S(1)}, f32[260,256]{0,1:T(8,128)S(1)}, u32[]{:S(2)}, u32[]{:S(2)}) collective-permute-start(f32[260,256]{0,1:T(8,128)S(1)} %pad_maximum_fusion.1), channel_id=1, source_target_pairs={{16,0},{32,16},{48,32},{64,48},{80,64},{96,80},{112,96},{128,112},... | collective-permute-start | bytes 798728 | tf_op jit(solution)/shard_map/ppermute | solution.py:27
  276.3 24.0 %all-to-all-start.2 = ((f32[16,1,4096]{2,1,0:T(1,128)}), f32[16,1,4096]{2,1,0:T(1,128)S(1)}, u32[]{:S(2)}, u32[]{:S(2)}) async-start(f32[16,1,4096]{2,1,0:T(1,128)} %reshape.180), calls=%async_computation.2 | async-start | bytes 524288 | tf_op jit(solution)/shard_map/all_to_all | solution.py:122
where the time goes:
time: 348 us; the launch traced here: 347 us
  matrix products  110 us (32%)
  local copies, waits for them, and re-layouts  106 us (30%)
  waiting for transfers between devices  59.9 us (17%)
  starting transfers between devices  34.2 us (10%)
  blocking collectives  23.9 us (7%)
  other arithmetic  6.98 us (2%)
  loops' own time  5.18 us (1%)
    gather x16, local copies, waits for them, and re-layouts, one_freq(): picked = freq_block[:, :, columns]  31.7 us
    dot_general x8, matrix products, one_freq(): jnp.einsum('pij,rpj->rpi', kern_imag, picked[1], precision=highest)  27 us
    dot_general x8, matrix products, one_freq(): jnp.einsum('pij,rpj->rpi', kern_imag, picked[0], precision=highest)  27 us
    dot_general x8, matrix products, one_freq(): jnp.einsum('pij,rpj->rpi', kern_real, picked[1], precision=highest)  26.3 us
    dot_general x8, matrix products, one_freq(): jnp.einsum('pij,rpj->rpi', kern_real, picked[0], precision=highest)  26.3 us
    all_to_all x1, blocking collectives, body(): lax.all_to_all(time_domain, 'freq', split_axis=0, concat_axis=2, tiled=True)  23.9 us
    dynamic_slice x32, local copies, waits for them, and re-layouts, body(): near_field = lax.map(one_freq, (laplace_real, laplace_imag, spectra))  20.6 us
    all_to_all x1, waiting for transfers between devices, body(): lax.all_to_all(near_field, 'freq', split_axis=3, concat_axis=0, tiled=True)  18.4 us
  transfers between devices with their start and end apart: 5, of which 5 were waited for; matrix products, arithmetic and copies ran while one was open for 0% of the time, Pallas kernels for 0%

commit v1 on v0

v1 whole, which is shorter than its diff:
```python
import functools

import jax
import jax.numpy as jnp
import ml_dtypes
import numpy as np
from jax import lax
from jax.experimental import pallas as pl
from jax.experimental.pallas import tpu as pltpu
from jax.sharding import PartitionSpec as P

MESH = pl.DeviceIdType.MESH
PATCH = 128
PATCH_DEV = 2
NEAR_MOST = 4
WIDTH = PATCH * PATCH_DEV
DECAY = 0.1
SMOOTH = 0.25
GEN_ROWS = 64


def split_bf16(table):
    high = table.astype(np.float32).astype(ml_dtypes.bfloat16)
    low = (table - high.astype(np.float64)).astype(np.float32).astype(ml_dtypes.bfloat16)
    return high, low


def transform_tables(steps):
    freq = np.arange(steps // 2)[:, None, None]
    part = np.arange(2)[None, :, None]
    time = np.arange(steps)[None, None, :]
    angle = ((2 * freq + 1) * time % (2 * steps)) * (np.pi / steps)
    waves = np.where(part == 0, np.cos(angle), np.sin(angle)).reshape(steps, steps)
    growth = DECAY ** (np.arange(steps) / steps)
    forward = waves * growth[None, :]
    inverse = waves.T * (2.0 / steps / growth)[:, None]
    return np.concatenate(split_bf16(forward) + split_bf16(inverse), axis=0)


def laplace_table(steps):
    angle = (2 * np.arange(steps // 2) + 1) * (np.pi / steps)
    zeta = DECAY ** (1.0 / steps) * np.exp(1j * angle)
    delta = (1 - zeta) + (1 - zeta) ** 2 / 2
    return np.stack([-delta.real * np.log2(np.e), delta.imag / (2 * np.pi)]).astype(np.float32)


def fit_even(function, degree):
    nodes = 0.125 + 0.125 * np.cos(np.pi * (np.arange(200) + 0.5) / 200)
    fitted = np.polynomial.chebyshev.Chebyshev.fit(nodes, function(np.sqrt(nodes)), degree, domain=[0, 0.25])
    return [float(c) for c in fitted.convert(kind=np.polynomial.Polynomial).coef]


SINE = fit_even(lambda f: np.sin(np.pi * f) / f, 4)
COSINE = fit_even(lambda f: np.cos(np.pi * f), 4)


def horner(coefficients, value):
    total = coefficients[-1] * value + coefficients[-2]
    for coefficient in coefficients[-3::-1]:
        total = total * value + coefficient
    return total


def halves(value):
    high = value.astype(jnp.bfloat16)
    return high, (value - high.astype(jnp.float32)).astype(jnp.bfloat16)


def dot(left, right):
    return jnp.dot(left, right, preferred_element_type=jnp.float32)


def kernel(
    parts,
    node_parts,
    x_hbm,
    table_hbm,
    coords_ref,
    weights_ref,
    near_ref,
    counts_ref,
    laplace_ref,
    out_hbm,
    x_vmem,
    table,
    send1,
    recv1,
    send2,
    halo,
    picked,
    send3,
    recv3,
    send4,
    recv4,
    out_vmem,
    places,
    distance,
    static,
    kern_high,
    kern_low,
    local_sem,
    send_sem,
    recv_sem,
    halo_send,
    halo_recv,
    place_send,
    place_recv,
):
    me = lax.axis_index("freq")
    node = lax.axis_index("node")
    steps = parts * 16
    fields = parts
    right = lax.rem(node + 1, node_parts)
    left = lax.rem(node + node_parts - 1, node_parts)
    order = sorted(range(1, parts), key=lambda k: -min(k, parts - k))
    peers = [lax.rem(me + k, parts) for k in order]
    mine = pl.ds(pl.multiple_of(me * 16, 16), 16)

    loads = [
        pltpu.make_async_copy(x_hbm.at[:, pl.ds(p * PATCH, PATCH)], x_vmem.at[p], local_sem.at[p])
        for p in range(PATCH_DEV)
    ]
    loads.append(pltpu.make_async_copy(table_hbm, table, local_sem.at[2]))
    for load in loads:
        load.start()
    barrier = pltpu.get_barrier_semaphore()
    for peer in peers:
        pl.semaphore_signal(barrier, inc=1, device_id={"freq": peer}, device_id_type=MESH)
    for side in (left, right):
        pl.semaphore_signal(barrier, inc=1, device_id={"node": side}, device_id_type=MESH)

    for p in range(PATCH_DEV):
        span = pl.ds(p * PATCH, PATCH)
        places[2 + p, 0:3, :] = coords_ref[:, span]
        places[2 + p, 3:4, :] = weights_ref[:, span]
        places[2 + p, 4:8, :] = jnp.zeros((4, PATCH), jnp.float32)
    for p in range(PATCH_DEV):
        loads[p].wait()
        for f in range(fields):
            send1[p, pl.ds(f * 16, 16), :] = x_vmem[p, pl.ds(f, 16, stride=fields), :]
        recv1[p, mine, :] = send1[p, mine, :]
    pl.semaphore_wait(barrier, parts + 1)

    def exchange(phase, p, source, target):
        for peer in peers:
            pltpu.make_async_remote_copy(
                src_ref=source.at[pl.ds(pl.multiple_of(peer * 16, 16), 16)],
                dst_ref=target.at[mine],
                send_sem=send_sem.at[phase, p],
                recv_sem=recv_sem.at[phase, p],
                device_id={"freq": peer},
                device_id_type=MESH,
            ).start()

    def whole(phase, p, source, target):
        rows = pl.ds(0, (parts - 1) * 16)
        return pltpu.make_async_remote_copy(
            src_ref=source.at[rows],
            dst_ref=target.at[rows],
            send_sem=send_sem.at[phase, p],
            recv_sem=recv_sem.at[phase, p],
            device_id={"freq": peers[0]},
            device_id_type=MESH,
        )

    place_copies = [
        pltpu.make_async_remote_copy(
            src_ref=places.at[pl.ds(2, 2)],
            dst_ref=places.at[pl.ds(slot, 2)],
            send_sem=place_send.at[slot // 4],
            recv_sem=place_recv.at[slot // 4],
            device_id={"node": side},
            device_id_type=MESH,
        )
        for side, slot in ((right, 0), (left, 4))
    ]
    for copy in place_copies:
        copy.start()
    for p in range(PATCH_DEV):
        exchange(0, p, send1.at[p], recv1.at[p])

    for copy in place_copies:
        copy.wait_recv()
    total_patches = PATCH_DEV * node_parts

    def slot_of(p, k):
        slot = lax.rem(near_ref[p, k] - (node - 1) * PATCH_DEV + total_patches, total_patches)
        return jnp.clip(slot, 0, 3 * PATCH_DEV - 1)

    slots = [[slot_of(p, k) for k in range(NEAR_MOST)] for p in range(PATCH_DEV)]
    for p in range(PATCH_DEV):
        for k in range(NEAR_MOST):
            column = places[slots[p][k]].T
            total = SMOOTH
            for c in range(3):
                apart = column[:, c : c + 1] - coords_ref[c : c + 1, p * PATCH : (p + 1) * PATCH]
                total = total + apart * apart
            inverse = lax.rsqrt(total)
            live = jnp.where(k < counts_ref[p], 1.0 / (4.0 * np.pi), 0.0)
            rows = pl.ds((p * NEAR_MOST + k) * PATCH, PATCH)
            distance[rows, :] = total * inverse
            static[rows, :] = (column[:, 3:4] * live) * inverse

    blocks = PATCH_DEV * NEAR_MOST * PATCH // GEN_ROWS

    def generate(step, carry):
        l = step // blocks
        block = step % blocks
        rows = pl.ds(pl.multiple_of(block * GEN_ROWS, GEN_ROWS), GEN_ROWS)
        radius = distance[rows, :]
        decaying = jnp.exp2(radius * laplace_ref[0, me * 8 + l]) * static[rows, :]
        turns = radius * laplace_ref[1, me * 8 + l]
        turns = turns - jnp.round(turns)
        square = turns * turns
        sine = horner(SINE, square) * turns
        cosine = horner([-c for c in COSINE], square)
        double = decaying * sine
        double = double + double
        real_high, real_low = halves(decaying - double * sine)
        imag_high, imag_low = halves(double * cosine)
        into = pl.ds(pl.multiple_of(step * GEN_ROWS, GEN_ROWS), GEN_ROWS)
        kern_high[into, 0:PATCH] = real_high
        kern_high[into, PATCH : 2 * PATCH] = imag_high
        kern_low[into, 0:PATCH] = real_low
        kern_low[into, PATCH : 2 * PATCH] = imag_low
        return carry

    lax.fori_loop(0, 8 * blocks, generate, 0)

    def transform(index, data):
        data_high, data_low = halves(data)
        table_high = table[pl.ds(2 * index * steps, steps), :]
        table_low = table[pl.ds((2 * index + 1) * steps, steps), :]
        first = dot(table_high, jnp.concatenate([data_high, data_low], axis=1))
        return first[:, :PATCH] + first[:, PATCH:] + dot(table_low, data_high)

    loads[2].wait()
    for p in range(PATCH_DEV):
        whole(0, p, send1.at[p], recv1.at[p]).wait_recv()
        send2[p] = transform(0, recv1[p])
        halo[2 + p, mine, :] = send2[p, mine, :]
        exchange(1, p, send2.at[p], halo.at[2 + p])

    halo_copies = []
    for p in range(PATCH_DEV):
        whole(1, p, send2.at[p], halo.at[2 + p]).wait_recv()
        for side, slot in ((right, 0), (left, 4)):
            copy = pltpu.make_async_remote_copy(
                src_ref=halo.at[2 + p],
                dst_ref=halo.at[slot + p],
                send_sem=halo_send.at[slot // 4, p],
                recv_sem=halo_recv.at[slot // 4, p],
                device_id={"node": side},
                device_id_type=MESH,
            )
            copy.start()
            halo_copies.append(copy)
    for copy in halo_copies:
        copy.wait_recv()

    for p in range(PATCH_DEV):
        for k in range(NEAR_MOST):
            picked[p * NEAR_MOST + k] = halo[slots[p][k]]
        for l in range(8):
            both = jnp.concatenate(
                [
                    jnp.concatenate(
                        [picked[p * NEAR_MOST + k, pl.ds(2 * l + ri, fields, stride=16), :] for k in range(NEAR_MOST)],
                        axis=1,
                    )
                    for ri in range(2)
                ],
                axis=0,
            )
            both_high, both_low = halves(both)
            rows = pl.ds((l * PATCH_DEV + p) * NEAR_MOST * PATCH, NEAR_MOST * PATCH)
            first = dot(jnp.concatenate([both_high, both_low], axis=0), kern_high[rows, :])
            total = first[: 2 * fields] + first[2 * fields :] + dot(both_high, kern_low[rows, :])
            send3[p, pl.ds(2 * l, fields, stride=16), :] = total[:fields, :PATCH] - total[fields:, PATCH:]
            send3[p, pl.ds(2 * l + 1, fields, stride=16), :] = total[fields:, :PATCH] + total[:fields, PATCH:]
        recv3[p, mine, :] = send3[p, mine, :]
        exchange(2, p, send3.at[p], recv3.at[p])

    for p in range(PATCH_DEV):
        whole(2, p, send3.at[p], recv3.at[p]).wait_recv()
        send4[p] = transform(1, recv3[p])
        recv4[p, mine, :] = send4[p, mine, :]
        exchange(3, p, send4.at[p], recv4.at[p])

    stores = []
    for p in range(PATCH_DEV):
        whole(3, p, send4.at[p], recv4.at[p]).wait_recv()
        for f in range(fields):
            out_vmem[p, pl.ds(f, 16, stride=fields), :] = recv4[p, pl.ds(f * 16, 16), :]
        store = pltpu.make_async_copy(out_vmem.at[p], out_hbm.at[:, pl.ds(p * PATCH, PATCH)], local_sem.at[p])
        store.start()
        stores.append(store)

    for copy in place_copies + halo_copies:
        copy.wait_send()
    for p in range(PATCH_DEV):
        whole(0, p, send1.at[p], recv1.at[p]).wait_send()
        whole(1, p, send2.at[p], halo.at[2 + p]).wait_send()
        whole(2, p, send3.at[p], recv3.at[p]).wait_send()
        whole(3, p, send4.at[p], recv4.at[p]).wait_send()
    for store in stores:
        store.wait()


def body(density, coords, weights, neighbours, counts):
    parts = lax.axis_size("freq")
    node_parts = lax.axis_size("node")
    times, fields, width = density.shape
    steps = times * parts
    assert times == 16 and fields == parts and width == WIDTH
    rows = times * fields
    vmem = pl.BlockSpec(memory_space=pltpu.VMEM)
    smem = pl.BlockSpec(memory_space=pltpu.SMEM)
    hbm = pl.BlockSpec(memory_space=pltpu.HBM)
    buffer = pltpu.VMEM((PATCH_DEV, steps, PATCH), jnp.float32)
    pairs = PATCH_DEV * NEAR_MOST * PATCH
    result = pl.pallas_call(
        functools.partial(kernel, parts, node_parts),
        out_shape=jax.ShapeDtypeStruct((rows, width), jnp.float32),
        in_specs=[hbm, hbm, vmem, vmem, smem, smem, smem],
        out_specs=pl.BlockSpec(memory_space=pl.ANY),
        scratch_shapes=[
            pltpu.VMEM((PATCH_DEV, rows, PATCH), jnp.float32),
            pltpu.VMEM((4 * steps, steps), jnp.bfloat16),
            buffer,
            buffer,
            buffer,
            pltpu.VMEM((3 * PATCH_DEV, steps, PATCH), jnp.float32),
            pltpu.VMEM((PATCH_DEV * NEAR_MOST, steps, PATCH), jnp.float32),
            buffer,
            buffer,
            buffer,
            buffer,
            pltpu.VMEM((PATCH_DEV, rows, PATCH), jnp.float32),
            pltpu.VMEM((3 * PATCH_DEV, 8, PATCH), jnp.float32),
            pltpu.VMEM((pairs, PATCH), jnp.float32),
            pltpu.VMEM((pairs, PATCH), jnp.float32),
            pltpu.VMEM((8 * pairs, 2 * PATCH), jnp.bfloat16),
            pltpu.VMEM((8 * pairs, 2 * PATCH), jnp.bfloat16),
            pltpu.SemaphoreType.DMA((3,)),
            pltpu.SemaphoreType.DMA((4, PATCH_DEV)),
            pltpu.SemaphoreType.DMA((4, PATCH_DEV)),
            pltpu.SemaphoreType.DMA((2, PATCH_DEV)),
            pltpu.SemaphoreType.DMA((2, PATCH_DEV)),
            pltpu.SemaphoreType.DMA((2,)),
            pltpu.SemaphoreType.DMA((2,)),
        ],
        compiler_params=pltpu.CompilerParams(
            collective_id=0, has_side_effects=True, vmem_limit_bytes=60_000_000
        ),
    )(
        density.reshape(rows, width),
        jnp.asarray(transform_tables(steps)),
        coords,
        weights.reshape(1, width),
        neighbours,
        counts,
        jnp.asarray(laplace_table(steps)),
    )
    return result.reshape(times, fields, width)


def solution(mesh):
    placed = (P("freq", None, "node"), P(None, "node"), P("node"), P("node", None), P("node"))
    return jax.shard_map(
        body, mesh=mesh, in_specs=placed, out_specs=P("freq", None, "node"), check_vma=False
    )
```

time: 348 us -> 74.3 us (0.21)
  the two profiles are of different devices: /device:TPU:24 before, /device:TPU:8 now
where the time goes in v1:
time: 74.3 us; the launch traced here: 74.1 us
  Pallas kernels  72.4 us (97%)
  local copies, waits for them, and re-layouts  1.67 us (2%)
    pallas_call x1, Pallas kernels, body(): pl.pallas_call(functools.partial(kernel, parts, node_parts), out_shape=ja...  72.4 us
    unnamed x1, local copies, waits for them, and re-layouts  1.67 us

profile of v1, /device:TPU:8, one launch (start us, length us, event | category | flops | bytes accessed | tf_op | source)
XLA Modules:
  0.0 74.1 jit_solution(17347810045425631919)
XLA Ops:
  0.0 72.4 %shard_map.73 = f32[256,256]{1,0:T(8,128)} custom-call(f32[256,256]{1,0:T(8,128)} %bitcast.4, bf16[1024,256]{1,0:T(8,128)(2,1)} %constant.4.clone.table_hbm, f32[3,256]{1,0:T(4,128)} %coords_ref.1, f32[1,256]{1,0:T(1,128)} %bitcast.5, s32[2,4]{1,0:T(2,128)} %near_ref.1, s32[2]{0:T(128)} %counts_ref.1, f32[2,128]{1,0:T(2,128)} %constant.5.clone.laplace_ref), custom_call_target="tpu_custom_call" | custom-call | tf_op jit(solution)/shard_map/pallas_call | solution.py:322
  72.4 1.7 %copy.9 = f32[16,16,256]{2,1,0:T(8,128)} copy(f32[16,16,256]{2,1,0:T(8,128)} %bitcast.3) | data formatting | bytes 524288

commit v2 on v1

v2 whole, which is shorter than its diff:
```python
import functools

import jax
import jax.numpy as jnp
import ml_dtypes
import numpy as np
from jax import lax
from jax.experimental import pallas as pl
from jax.experimental.pallas import tpu as pltpu
from jax.sharding import PartitionSpec as P

MESH = pl.DeviceIdType.MESH
PATCH = 128
PATCH_DEV = 2
NEAR_MOST = 4
WIDTH = PATCH * PATCH_DEV
DECAY = 0.1
SMOOTH = 0.25
GEN_ROWS = 64


def split_bf16(table):
    high = table.astype(np.float32).astype(ml_dtypes.bfloat16)
    low = (table - high.astype(np.float64)).astype(np.float32).astype(ml_dtypes.bfloat16)
    return high, low


def transform_tables(steps):
    freq = np.arange(steps // 2)[:, None, None]
    part = np.arange(2)[None, :, None]
    time = np.arange(steps)[None, None, :]
    angle = ((2 * freq + 1) * time % (2 * steps)) * (np.pi / steps)
    waves = np.where(part == 0, np.cos(angle), np.sin(angle)).reshape(steps, steps)
    waves = waves.reshape(steps // 16, 2, 8, steps).transpose(1, 0, 2, 3).reshape(steps, steps)
    growth = DECAY ** (np.arange(steps) / steps)
    forward = waves * growth[None, :]
    inverse = waves.T * (2.0 / steps / growth)[:, None]
    return np.concatenate(split_bf16(forward) + split_bf16(inverse), axis=0)


def laplace_table(steps):
    angle = (2 * np.arange(steps // 2) + 1) * (np.pi / steps)
    zeta = DECAY ** (1.0 / steps) * np.exp(1j * angle)
    delta = (1 - zeta) + (1 - zeta) ** 2 / 2
    return np.stack([-delta.real * np.log2(np.e), delta.imag / (2 * np.pi)]).astype(np.float32)


def fit_even(function, degree):
    nodes = 0.125 + 0.125 * np.cos(np.pi * (np.arange(200) + 0.5) / 200)
    fitted = np.polynomial.chebyshev.Chebyshev.fit(nodes, function(np.sqrt(nodes)), degree, domain=[0, 0.25])
    return [float(c) for c in fitted.convert(kind=np.polynomial.Polynomial).coef]


SINE = fit_even(lambda f: np.sin(np.pi * f) / f, 4)
COSINE = fit_even(lambda f: np.cos(np.pi * f), 4)


def horner(coefficients, value):
    total = coefficients[-1] * value + coefficients[-2]
    for coefficient in coefficients[-3::-1]:
        total = total * value + coefficient
    return total


def halves(value):
    high = value.astype(jnp.bfloat16)
    return high, (value - high.astype(jnp.float32)).astype(jnp.bfloat16)


def dot(left, right):
    return jnp.dot(left, right, preferred_element_type=jnp.float32)


def kernel(
    parts,
    node_parts,
    x_hbm,
    table_hbm,
    coords_hbm,
    weights_hbm,
    near_hbm,
    counts_hbm,
    laplace_hbm,
    out_ref,
    x_vmem,
    table,
    coords_ref,
    weights_ref,
    near_ref,
    counts_ref,
    laplace_ref,
    send1,
    recv1,
    send2,
    halo_first,
    halo_second,
    picked,
    send3,
    recv3,
    send4,
    recv4,
    places,
    distance,
    static,
    kern_high,
    kern_low,
    local_sem,
    chain_sem,
    send_sem,
    recv_sem,
    half_send,
    half_recv,
    halo_send,
    halo_recv,
    place_send,
    place_recv,
):
    halo = (halo_first, halo_second)
    me = lax.axis_index("freq")
    node = lax.axis_index("node")
    steps = parts * 16
    fields = parts
    reach = parts // 4
    right = lax.rem(node + 1, node_parts)
    left = lax.rem(node + node_parts - 1, node_parts)

    def peers_of(order):
        return [lax.rem(me + k, parts) for k in order]

    def by_hops(first, last):
        order = [k for k in range(1, parts) if first <= min(k, parts - k) <= last]
        return peers_of(sorted(order, key=lambda k: -min(k, parts - k)))

    near_peers = by_hops(1, reach)
    far_peers = by_hops(reach + 1, 2 * reach)
    peers = far_peers + near_peers
    chain_peers = peers_of((reach, parts - reach))

    loads = [
        pltpu.make_async_copy(x_hbm.at[:, pl.ds(p * PATCH, PATCH)], x_vmem.at[p], local_sem.at[p])
        for p in range(PATCH_DEV)
    ]
    for source, target in (
        (coords_hbm, coords_ref),
        (weights_hbm, weights_ref),
        (near_hbm, near_ref),
        (counts_hbm, counts_ref),
        (laplace_hbm, laplace_ref),
        (table_hbm, table),
    ):
        loads.append(pltpu.make_async_copy(source, target, local_sem.at[len(loads)]))
    for load in loads:
        load.start()
    barrier = pltpu.get_barrier_semaphore()
    for peer in near_peers:
        pl.semaphore_signal(barrier, inc=1, device_id={"freq": peer}, device_id_type=MESH)
    for side in (left, right):
        pl.semaphore_signal(barrier, inc=1, device_id={"node": side}, device_id_type=MESH)

    def block(index, rows):
        return pl.ds(pl.multiple_of(index * rows, rows), rows)

    mine = block(me, 16)
    for p in range(PATCH_DEV):
        loads[p].wait()
        for f in range(fields):
            send1[p, pl.ds(f * 16, 16), :] = x_vmem[p, pl.ds(f, 16, stride=fields), :]
        recv1[p, mine, :] = send1[p, mine, :]
    for load in loads[2:7]:
        load.wait()
    for p in range(PATCH_DEV):
        span = pl.ds(p * PATCH, PATCH)
        places[2 + p, 0:3, :] = coords_ref[:, span]
        places[2 + p, 3:4, :] = weights_ref[:, span]
        places[2 + p, 4:8, :] = jnp.zeros((4, PATCH), jnp.float32)
    pl.semaphore_wait(barrier, len(near_peers) + 2)

    def push(peer, source, target, rows, sends, receives):
        pltpu.make_async_remote_copy(
            src_ref=source.at[block(peer, rows)],
            dst_ref=target.at[block(me, rows)],
            send_sem=sends,
            recv_sem=receives,
            device_id={"freq": peer},
            device_id_type=MESH,
        ).start()

    def whole(source, target, rows, sends, receives):
        span = pl.ds(0, (parts - 1) * rows)
        return pltpu.make_async_remote_copy(
            src_ref=source.at[span],
            dst_ref=target.at[span],
            send_sem=sends,
            recv_sem=receives,
            device_id={"freq": peers[0]},
            device_id_type=MESH,
        )

    def full(phase, p):
        source, target = ((send1, recv1), (send4, recv4))[phase]
        return source.at[p], target.at[p], 16, send_sem.at[phase, p], recv_sem.at[phase, p]

    def part(phase, p, h):
        source, target = ((send2.at[p, h], halo[h].at[2 + p]), (send3.at[p, h], recv3.at[p, h]))[phase]
        return source, target, 8, half_send.at[phase, p, h], half_recv.at[phase, p, h]

    for peer in chain_peers:
        pl.semaphore_signal(chain_sem, inc=1, device_id={"freq": peer}, device_id_type=MESH)
    place_copies = [
        pltpu.make_async_remote_copy(
            src_ref=places.at[pl.ds(2, 2)],
            dst_ref=places.at[pl.ds(slot, 2)],
            send_sem=place_send.at[slot // 4],
            recv_sem=place_recv.at[slot // 4],
            device_id={"node": side},
            device_id_type=MESH,
        )
        for side, slot in ((right, 0), (left, 4))
    ]
    for copy in place_copies:
        copy.start()
    for p in range(PATCH_DEV):
        for peer in near_peers:
            push(peer, *full(0, p))
    pl.semaphore_wait(chain_sem, 2)
    for p in range(PATCH_DEV):
        for peer in far_peers:
            push(peer, *full(0, p))

    for copy in place_copies:
        copy.wait_recv()
    total_patches = PATCH_DEV * node_parts

    def slot_of(p, k):
        slot = lax.rem(near_ref[p, k] - (node - 1) * PATCH_DEV + total_patches, total_patches)
        return jnp.clip(slot, 0, 3 * PATCH_DEV - 1)

    slots = [[slot_of(p, k) for k in range(NEAR_MOST)] for p in range(PATCH_DEV)]
    for p in range(PATCH_DEV):
        for k in range(NEAR_MOST):
            column = places[slots[p][k]].T
            total = SMOOTH
            for c in range(3):
                apart = column[:, c : c + 1] - coords_ref[c : c + 1, p * PATCH : (p + 1) * PATCH]
                total = total + apart * apart
            inverse = lax.rsqrt(total)
            live = jnp.where(k < counts_ref[p], 1.0 / (4.0 * np.pi), 0.0)
            rows = pl.ds((p * NEAR_MOST + k) * PATCH, PATCH)
            distance[rows, :] = total * inverse
            static[rows, :] = (column[:, 3:4] * live) * inverse

    blocks = PATCH_DEV * NEAR_MOST * PATCH // GEN_ROWS

    def generate(step, carry):
        l = step // blocks
        rows = block(step % blocks, GEN_ROWS)
        radius = distance[rows, :]
        decaying = jnp.exp2(radius * laplace_ref[0, me * 8 + l]) * static[rows, :]
        turns = radius * laplace_ref[1, me * 8 + l]
        turns = turns - jnp.round(turns)
        square = turns * turns
        sine = horner(SINE, square) * turns
        cosine = horner([-c for c in COSINE], square)
        double = decaying * sine
        double = double + double
        real_high, real_low = halves(decaying - double * sine)
        imag_high, imag_low = halves(double * cosine)
        into = block(step, GEN_ROWS)
        kern_high[into, 0:PATCH] = real_high
        kern_high[into, PATCH : 2 * PATCH] = imag_high
        kern_low[into, 0:PATCH] = real_low
        kern_low[into, PATCH : 2 * PATCH] = imag_low
        return carry

    lax.fori_loop(0, 4 * blocks, generate, 0)

    def transform(index, data):
        data_high, data_low = halves(data)
        table_high = table[pl.ds(2 * index * steps, steps), :]
        table_low = table[pl.ds((2 * index + 1) * steps, steps), :]
        first = dot(table_high, jnp.concatenate([data_high, data_low], axis=1))
        return first[:, :PATCH] + first[:, PATCH:] + dot(table_low, data_high)

    half_rows = parts * 8
    loads[7].wait()
    for p in range(PATCH_DEV):
        whole(*full(0, p)).wait_recv()
        spectrum = transform(0, recv1[p])
        for h in range(2):
            send2[p, h] = spectrum[h * half_rows : (h + 1) * half_rows]
            halo[h][2 + p, block(me, 8), :] = send2[p, h, block(me, 8), :]
        for peer in peers:
            push(peer, *part(0, p, 0))
    for p in range(PATCH_DEV):
        for peer in peers:
            push(peer, *part(0, p, 1))

    lax.fori_loop(4 * blocks, 8 * blocks, generate, 0)

    halo_copies = {}

    def spread(p, h):
        whole(*part(0, p, h)).wait_recv()
        for side, slot in ((right, 0), (left, 4)):
            copy = pltpu.make_async_remote_copy(
                src_ref=halo[h].at[2 + p],
                dst_ref=halo[h].at[slot + p],
                send_sem=halo_send.at[slot // 4, p, h],
                recv_sem=halo_recv.at[slot // 4, p, h],
                device_id={"node": side},
                device_id_type=MESH,
            )
            copy.start()
            halo_copies[slot, p, h] = copy

    def near_field(h):
        for p in range(PATCH_DEV):
            for slot in (0, 4):
                halo_copies[slot, p, h].wait_recv()
        for p in range(PATCH_DEV):
            for k in range(NEAR_MOST):
                picked[h, p * NEAR_MOST + k] = halo[h][slots[p][k]]
            for l in range(4):
                both = jnp.concatenate(
                    [
                        jnp.concatenate(
                            [
                                picked[h, p * NEAR_MOST + k, pl.ds(2 * l + ri, fields, stride=8), :]
                                for k in range(NEAR_MOST)
                            ],
                            axis=1,
                        )
                        for ri in range(2)
                    ],
                    axis=0,
                )
                both_high, both_low = halves(both)
                start = ((4 * h + l) * PATCH_DEV + p) * NEAR_MOST * PATCH
                rows = pl.ds(start, NEAR_MOST * PATCH)
                first = dot(jnp.concatenate([both_high, both_low], axis=0), kern_high[rows, :])
                total = first[: 2 * fields] + first[2 * fields :] + dot(both_high, kern_low[rows, :])
                send3[p, h, pl.ds(2 * l, fields, stride=8), :] = total[:fields, :PATCH] - total[fields:, PATCH:]
                send3[p, h, pl.ds(2 * l + 1, fields, stride=8), :] = total[fields:, :PATCH] + total[:fields, PATCH:]
            recv3[p, h, block(me, 8), :] = send3[p, h, block(me, 8), :]
            for peer in peers:
                push(peer, *part(1, p, h))

    spread(0, 0)
    spread(1, 0)
    spread(0, 1)
    near_field(0)
    spread(1, 1)
    near_field(1)

    for p in range(PATCH_DEV):
        for h in range(2):
            whole(*part(1, p, h)).wait_recv()
        send4[p] = transform(1, jnp.concatenate([recv3[p, 0], recv3[p, 1]], axis=0))
        recv4[p, mine, :] = send4[p, mine, :]
        for peer in peers:
            push(peer, *full(1, p))

    for p in range(PATCH_DEV):
        whole(*full(1, p)).wait_recv()
        for f in range(fields):
            out_ref[p, pl.ds(f, 16, stride=fields), :] = recv4[p, pl.ds(f * 16, 16), :]

    for copy in place_copies + list(halo_copies.values()):
        copy.wait_send()
    for p in range(PATCH_DEV):
        whole(*full(0, p)).wait_send()
        whole(*full(1, p)).wait_send()
        for h in range(2):
            whole(*part(0, p, h)).wait_send()
            whole(*part(1, p, h)).wait_send()


def body(density, coords, weights, neighbours, counts):
    parts = lax.axis_size("freq")
    node_parts = lax.axis_size("node")
    times, fields, width = density.shape
    steps = times * parts
    assert times == 16 and fields == parts and width == WIDTH
    rows = times * fields
    hbm = pl.BlockSpec(memory_space=pltpu.HBM)
    buffer = pltpu.VMEM((PATCH_DEV, steps, PATCH), jnp.float32)
    half_buffer = pltpu.VMEM((PATCH_DEV, 2, steps // 2, PATCH), jnp.float32)
    pairs = PATCH_DEV * NEAR_MOST * PATCH
    operands = [
        density.reshape(rows, width),
        jnp.asarray(transform_tables(steps)),
        coords,
        weights.reshape(1, width),
        neighbours,
        counts,
        jnp.asarray(laplace_table(steps)),
    ]
    operands = [pltpu.with_memory_space_constraint(operand, pltpu.HBM) for operand in operands]
    result = pl.pallas_call(
        functools.partial(kernel, parts, node_parts),
        out_shape=jax.ShapeDtypeStruct((PATCH_DEV, rows, PATCH), jnp.float32),
        in_specs=[hbm] * len(operands),
        out_specs=pl.BlockSpec(memory_space=pltpu.VMEM),
        scratch_shapes=[
            pltpu.VMEM((PATCH_DEV, rows, PATCH), jnp.float32),
            pltpu.VMEM((4 * steps, steps), jnp.bfloat16),
            pltpu.VMEM((3, width), jnp.float32),
            pltpu.VMEM((1, width), jnp.float32),
            pltpu.SMEM((PATCH_DEV, NEAR_MOST), jnp.int32),
            pltpu.SMEM((PATCH_DEV,), jnp.int32),
            pltpu.SMEM((2, steps // 2), jnp.float32),
            buffer,
            buffer,
            half_buffer,
            pltpu.VMEM((3 * PATCH_DEV, steps // 2, PATCH), jnp.float32),
            pltpu.VMEM((3 * PATCH_DEV, steps // 2, PATCH), jnp.float32),
            pltpu.VMEM((2, PATCH_DEV * NEAR_MOST, steps // 2, PATCH), jnp.float32),
            half_buffer,
            half_buffer,
            buffer,
            buffer,
            pltpu.VMEM((3 * PATCH_DEV, 8, PATCH), jnp.float32),
            pltpu.VMEM((pairs, PATCH), jnp.float32),
            pltpu.VMEM((pairs, PATCH), jnp.float32),
            pltpu.VMEM((8 * pairs, 2 * PATCH), jnp.bfloat16),
            pltpu.VMEM((8 * pairs, 2 * PATCH), jnp.bfloat16),
            pltpu.SemaphoreType.DMA((8,)),
            pltpu.SemaphoreType.REGULAR,
            pltpu.SemaphoreType.DMA((2, PATCH_DEV)),
            pltpu.SemaphoreType.DMA((2, PATCH_DEV)),
            pltpu.SemaphoreType.DMA((2, PATCH_DEV, 2)),
            pltpu.SemaphoreType.DMA((2, PATCH_DEV, 2)),
            pltpu.SemaphoreType.DMA((2, PATCH_DEV, 2)),
            pltpu.SemaphoreType.DMA((2, PATCH_DEV, 2)),
            pltpu.SemaphoreType.DMA((2,)),
            pltpu.SemaphoreType.DMA((2,)),
        ],
        compiler_params=pltpu.CompilerParams(
            collective_id=0, has_side_effects=True, vmem_limit_bytes=40_000_000
        ),
    )(*operands)
    return jnp.swapaxes(result.reshape(PATCH_DEV, times, fields, PATCH), 0, 1).swapaxes(1, 2).reshape(times, fields, width)


def solution(mesh):
    placed = (P("freq", None, "node"), P(None, "node"), P("node"), P("node", None), P("node"))
    return jax.shard_map(
        body, mesh=mesh, in_specs=placed, out_specs=P("freq", None, "node"), check_vma=False
    )
```

time: 74.3 us -> 68.6 us (0.923)
  the two profiles are of different devices: /device:TPU:8 before, /device:TPU:23 now
where the time goes in v2:
time: 68.6 us; the launch traced here: 68.5 us
  Pallas kernels  67.7 us (99%)
  local copies, waits for them, and re-layouts  0.73 us (1%)
    pallas_call x1, Pallas kernels, body(): pl.pallas_call(functools.partial(kernel, parts, node_parts), out_shape=ja...  67.7 us

profile of v2, /device:TPU:23, one launch (start us, length us, event | category | flops | bytes accessed | tf_op | source)
XLA Modules:
  0.0 68.5 jit_solution(13643521037477095886)
XLA Ops:
  0.0 67.7 %shard_map.73 = f32[2,256,128]{2,1,0:T(8,128)S(1)} custom-call(f32[256,256]{1,0:T(8,128)} %bitcast.10, bf16[1024,256]{1,0:T(8,128)(2,1)} %constant.4.clone.table_hbm, f32[3,256]{1,0:T(4,128)} %coords_hbm.1, f32[1,256]{1,0:T(1,128)} %bitcast.11, s32[2,4]{1,0:T(2,128)} %near_hbm.1, s32[2]{0:T(128)} %counts_hbm.1, f32[2,128]{1,0:T(2,128)} %constant.5.clone.laplace_hbm), custom_call_target="tpu_custom_call" | custom-call | tf_op jit(solution)/shard_map/pallas_call | solution.py:399
  67.7 0.7 %copy.11 = f32[2,16,2,8,128]{4,3,0,2,1:T(8,128)} copy(f32[2,16,2,8,128]{4,3,2,1,0:T(8,128)S(1)} %bitcast.9) | data formatting | bytes 524288 | tf_op jit(solution)/shard_map/reshape | solution.py:442

commit v3 on v2

v3 whole, which is shorter than its diff:
```python
import functools
import math

import jax
import jax.numpy as jnp
import ml_dtypes
import numpy as np
from jax import lax
from jax.experimental import pallas as pl
from jax.experimental.pallas import tpu as pltpu
from jax.sharding import PartitionSpec as P

MESH = pl.DeviceIdType.MESH
PATCH = 128
PATCH_DEV = 2
NEAR_MOST = 4
OFFSETS = 5
WIDTH = PATCH * PATCH_DEV
DECAY = 0.1
SMOOTH = 0.25
GEN_ROWS = 64


def split_bf16(table):
    high = table.astype(np.float32).astype(ml_dtypes.bfloat16)
    low = (table - high.astype(np.float64)).astype(np.float32).astype(ml_dtypes.bfloat16)
    return high, low


def transform_tables(steps):
    freq = np.arange(steps // 2)[:, None, None]
    part = np.arange(2)[None, :, None]
    time = np.arange(steps)[None, None, :]
    angle = ((2 * freq + 1) * time % (2 * steps)) * (np.pi / steps)
    waves = np.where(part == 0, np.cos(angle), np.sin(angle)).reshape(steps, steps)
    growth = DECAY ** (np.arange(steps) / steps)
    forward = waves * growth[None, :]
    inverse = waves.T * (2.0 / steps / growth)[:, None]
    return np.concatenate(split_bf16(forward) + split_bf16(inverse), axis=0)


def laplace_table(steps):
    angle = (2 * np.arange(steps // 2) + 1) * (np.pi / steps)
    zeta = DECAY ** (1.0 / steps) * np.exp(1j * angle)
    delta = (1 - zeta) + (1 - zeta) ** 2 / 2
    return np.stack([-delta.real * np.log2(np.e), delta.imag / (2 * np.pi)]).astype(np.float32)


def fit_even(function, degree):
    nodes = 0.125 + 0.125 * np.cos(np.pi * (np.arange(200) + 0.5) / 200)
    fitted = np.polynomial.chebyshev.Chebyshev.fit(nodes, function(np.sqrt(nodes)), degree, domain=[0, 0.25])
    return [float(c) for c in fitted.convert(kind=np.polynomial.Polynomial).coef]


SINE = fit_even(lambda f: np.sin(np.pi * f) / f, 4)
COSINE = fit_even(lambda f: np.cos(np.pi * f), 4)


def horner(coefficients, value):
    total = coefficients[-1] * value + coefficients[-2]
    for coefficient in coefficients[-3::-1]:
        total = total * value + coefficient
    return total


def halves(value):
    high = value.astype(jnp.bfloat16)
    return high, (value - high.astype(jnp.float32)).astype(jnp.bfloat16)


def dot(left, right):
    return jnp.dot(left, right, preferred_element_type=jnp.float32)


def kernel(
    parts,
    x_hbm,
    table_hbm,
    coords_hbm,
    weights_hbm,
    near_hbm,
    counts_hbm,
    laplace_hbm,
    out_ref,
    x_vmem,
    table,
    coords_ref,
    weights_ref,
    near_ref,
    counts_ref,
    laplace_ref,
    send1,
    relay,
    recv1,
    send2,
    halo,
    send3,
    recv3,
    send4,
    recv4,
    place_own,
    places,
    distance,
    static,
    kern_high,
    kern_low,
    local_sem,
    chain_sem,
    relay_send,
    relay_recv,
    send_sem,
    recv_sem,
    share_recv,
    halo_send,
    halo_recv,
    spread_send,
    spread_recv,
    place_send,
    place_recv,
):
    z = lax.axis_index("freq")
    node = lax.axis_index("node")
    core = lax.rem(node, 2)
    column = node // 2
    side = math.isqrt(parts)
    steps = parts * 16
    fields = parts
    reach = parts // 4
    total_patches = 2 * parts * PATCH_DEV
    diagonal = z == column

    def shifted(k):
        return lax.rem(z + k, parts)

    def moved(dy, dx):
        return lax.rem(column // side + dy, side) * side + lax.rem(lax.rem(column, side) + dx, side)

    def hops(k, count):
        return min(k, count - k)

    planar = [(dy, dx) for dy in range(side) for dx in range(side) if dy or dx]
    planar.sort(key=lambda move: hops(move[0], side) + hops(move[1], side))
    near_first = [moved(dy, dx) for dy, dx in planar]
    far_first = near_first[::-1]
    along = sorted(range(1, parts), key=lambda k: -hops(k, parts))
    right = {"node": node + 1 - 2 * core, "freq": lax.rem(z + core, parts)}
    left = {"node": node + 1 - 2 * core, "freq": lax.rem(z + parts - 1 + core, parts)}

    barrier = pltpu.get_barrier_semaphore()
    greeted = [{"freq": shifted(k)} for k in along if hops(k, parts) <= reach]
    greeted += [{"node": 2 * other + core} for other in near_first] + [left, right]
    for device in greeted:
        pl.semaphore_signal(barrier, inc=1, device_id=device, device_id_type=MESH)

    loads = [
        pltpu.make_async_copy(x_hbm.at[:, pl.ds(p * PATCH, PATCH)], x_vmem.at[p], local_sem.at[p])
        for p in range(PATCH_DEV)
    ]
    for source, target in (
        (coords_hbm, coords_ref),
        (weights_hbm, weights_ref),
        (near_hbm, near_ref),
        (counts_hbm, counts_ref),
        (laplace_hbm, laplace_ref),
        (table_hbm, table),
    ):
        loads.append(pltpu.make_async_copy(source, target, local_sem.at[len(loads)]))
    for load in loads:
        load.start()

    def block(index):
        return pl.ds(pl.multiple_of(index * 16, 16), 16)

    for p in range(PATCH_DEV):
        loads[p].wait()
        for f in range(fields):
            send1[p, pl.ds(f * 16, 16), :] = x_vmem[p, pl.ds(f, 16, stride=fields), :]
        relay[p, block(column), :] = send1[p, block(column), :]
    for load in loads[2:7]:
        load.wait()
    lanes = lax.broadcasted_iota(jnp.int32, (8, PATCH), 1)
    masks = jnp.zeros((8, PATCH), jnp.float32)
    for p in range(PATCH_DEV):
        span = pl.ds(p * PATCH, PATCH)
        place_own[4 * p : 4 * p + 3, :] = coords_ref[:, span]
        place_own[4 * p + 3 : 4 * p + 4, :] = weights_ref[:, span]
        for o in range(OFFSETS):
            wanted = lax.rem(node * PATCH_DEV + p + o - OFFSETS // 2 + total_patches, total_patches)
            mask = jnp.float32(0)
            for k in range(NEAR_MOST):
                used = jnp.logical_and(near_ref[p, k] == wanted, k < counts_ref[p])
                mask = mask + jnp.where(used, 1.0, 0.0)
            masks = jnp.where(lanes == p * OFFSETS + o, mask, masks)
    place_own[8:16, :] = masks
    pl.semaphore_wait(barrier, len(greeted))

    def push(device, source, target, sends, receives):
        pltpu.make_async_remote_copy(
            src_ref=source,
            dst_ref=target,
            send_sem=sends,
            recv_sem=receives,
            device_id=device,
            device_id_type=MESH,
        ).start()

    def pending(source, target, count, sends, receives):
        span = pl.ds(0, count * 16)
        return pltpu.make_async_remote_copy(
            src_ref=source.at[span],
            dst_ref=target.at[span],
            send_sem=sends,
            recv_sem=receives,
            device_id=right,
            device_id_type=MESH,
        )

    def stage(index, p):
        source, target = (
            (relay.at[p], recv1.at[p]),
            (send2.at[p], halo.at[2 + p]),
            (send3.at[p], recv3.at[p]),
            (send4.at[p], recv4.at[p]),
        )[index]
        return source, target, send_sem.at[index, p], recv_sem.at[index, p]

    def rest(index, p, count):
        source, target, sends, receives = stage(index, p)
        return pending(source, target, count, sends, receives)

    for k in (reach, parts - reach):
        pl.semaphore_signal(chain_sem, inc=1, device_id={"freq": shifted(k)}, device_id_type=MESH)
    def place_copy(index):
        return pltpu.make_async_remote_copy(
            src_ref=place_own,
            dst_ref=places.at[1],
            send_sem=spread_send.at[index],
            recv_sem=spread_recv,
            device_id={"node": 2 * near_first[index] + core},
            device_id_type=MESH,
        )

    @pl.when(diagonal)
    def _():
        for index in range(parts - 1):
            place_copy(index).start()
        places[1] = place_own[...]

    for p in range(PATCH_DEV):
        for other in near_first:
            push(
                {"node": 2 * other + core},
                send1.at[p, block(other)],
                relay.at[p, block(column)],
                relay_send.at[p],
                relay_recv.at[p, column],
            )

    pl.semaphore_wait(chain_sem, 2)

    def forward(p, source):
        _, _, sends, receives = stage(0, p)
        push({"freq": source}, relay.at[p, block(source)], recv1.at[p, block(z)], sends, receives)

    def keep(p):
        @pl.when(jnp.logical_not(diagonal))
        def _():
            arrived(p, z)

        recv1[p, block(z), :] = relay[p, block(z), :]

    def arrived(p, source):
        pltpu.make_async_remote_copy(
            src_ref=relay.at[p, block(source)],
            dst_ref=relay.at[p, block(source)],
            send_sem=relay_send.at[p],
            recv_sem=relay_recv.at[p, source],
            device_id=right,
            device_id_type=MESH,
        ).wait_recv()

    def forward_as_arrived(p):
        @pl.when(jnp.logical_not(diagonal))
        def _():
            forward(p, column)

        for other in near_first:

            @pl.when(other != z)
            def _(other=other):
                arrived(p, other)
                forward(p, other)

    def forward_far_first(p):
        for k in along:
            source = shifted(k)

            @pl.when(source != column)
            def _(source=source):
                arrived(p, source)

            forward(p, source)

    forward_as_arrived(0)

    @pl.when(jnp.logical_not(diagonal))
    def _():
        place_copy(0).wait_recv()

    place_copies = [
        pltpu.make_async_remote_copy(
            src_ref=places.at[1],
            dst_ref=places.at[slot],
            send_sem=place_send.at[slot // 2],
            recv_sem=place_recv.at[slot // 2],
            device_id=device,
            device_id_type=MESH,
        )
        for device, slot in ((right, 0), (left, 2))
    ]
    for copy in place_copies:
        copy.start()
    forward_far_first(1)
    for p in range(PATCH_DEV):
        keep(p)
    for copy in place_copies:
        copy.wait_recv()

    turned = [places[index].T for index in range(3)]
    for p in range(PATCH_DEV):
        for o in range(OFFSETS):
            other = turned[(p + o) // PATCH_DEV]
            first = 4 * ((p + o) % PATCH_DEV)
            total = SMOOTH
            for c in range(3):
                apart = other[:, first + c : first + c + 1] - places[1, 4 * p + c : 4 * p + c + 1, :]
                total = total + apart * apart
            inverse = lax.rsqrt(total)
            lane = p * OFFSETS + o
            scale = places[1, 8:9, lane : lane + 1] * (1.0 / (4.0 * np.pi))
            rows = pl.ds((p * OFFSETS + o) * PATCH, PATCH)
            distance[rows, :] = total * inverse
            static[rows, :] = (other[:, first + 3 : first + 4] * scale) * inverse

    blocks = PATCH_DEV * OFFSETS * PATCH // GEN_ROWS

    def generate(step, carry):
        l = step // blocks
        rows = pl.ds(pl.multiple_of(step % blocks * GEN_ROWS, GEN_ROWS), GEN_ROWS)
        radius = distance[rows, :]
        decaying = jnp.exp2(radius * laplace_ref[0, column * 8 + l]) * static[rows, :]
        turns = radius * laplace_ref[1, column * 8 + l]
        turns = turns - jnp.round(turns)
        square = turns * turns
        sine = horner(SINE, square) * turns
        cosine = horner([-c for c in COSINE], square)
        double = decaying * sine
        double = double + double
        real_high, real_low = halves(decaying - double * sine)
        imag_high, imag_low = halves(double * cosine)
        into = pl.ds(pl.multiple_of(step * GEN_ROWS, GEN_ROWS), GEN_ROWS)
        kern_high[into, 0:PATCH] = real_high
        kern_high[into, PATCH : 2 * PATCH] = imag_high
        kern_low[into, 0:PATCH] = real_low
        kern_low[into, PATCH : 2 * PATCH] = imag_low
        return carry

    lax.fori_loop(0, 4 * blocks, generate, 0)

    def transform(index, data):
        data_high, data_low = halves(data)
        table_high = table[pl.ds(2 * index * steps, steps), :]
        table_low = table[pl.ds((2 * index + 1) * steps, steps), :]
        first = dot(table_high, jnp.concatenate([data_high, data_low], axis=1))
        return first[:, :PATCH] + first[:, PATCH:] + dot(table_low, data_high)

    def across(index, p, receives=None):
        source, target, sends, arrivals = stage(index, p)
        receives = arrivals if receives is None else receives
        for other in far_first:
            push({"node": 2 * other + core}, source.at[block(other)], target.at[block(column)], sends, receives)

    def forward_transform(p, receives=None):
        rest(0, p, parts - 1).wait_recv()
        send2[p] = transform(0, recv1[p])
        halo[2 + p, block(column), :] = send2[p, block(column), :]
        across(1, p, receives)

    sides = ((right, 0), (left, 4))

    def halo_copy(p, slot, device):
        return pltpu.make_async_remote_copy(
            src_ref=halo.at[2 + p],
            dst_ref=halo.at[slot + p],
            send_sem=halo_send.at[slot // 4, p],
            recv_sem=halo_recv.at[slot // 4, p],
            device_id=device,
            device_id_type=MESH,
        )

    halo_copies = [halo_copy(p, slot, device) for p in range(PATCH_DEV) for device, slot in sides]

    def share_chunk(p, index):
        for device, slot in sides:
            push(
                device,
                halo.at[2 + p, block(index)],
                halo.at[slot + p, block(index)],
                halo_send.at[slot // 4, p],
                halo_recv.at[slot // 4, p],
            )

    loads[7].wait()
    forward_transform(0)
    forward_transform(1, share_recv.at[column])
    share_chunk(1, column)
    lax.fori_loop(4 * blocks, 6 * blocks, generate, 0)
    rest(1, 0, parts - 1).wait_recv()
    for copy in halo_copies[:2]:
        copy.start()
    for other in near_first:
        pltpu.make_async_remote_copy(
            src_ref=halo.at[3, block(other)],
            dst_ref=halo.at[3, block(other)],
            send_sem=send_sem.at[1, 1],
            recv_sem=share_recv.at[other],
            device_id=right,
            device_id_type=MESH,
        ).wait_recv()
        share_chunk(1, other)
    lax.fori_loop(6 * blocks, 8 * blocks, generate, 0)
    for copy in halo_copies:
        copy.wait_recv()

    for p in range(PATCH_DEV):
        for l in range(8):
            both = jnp.concatenate(
                [
                    jnp.concatenate(
                        [halo[p + o, pl.ds(2 * l + ri, fields, stride=16), :] for o in range(OFFSETS)],
                        axis=1,
                    )
                    for ri in range(2)
                ],
                axis=0,
            )
            both_high, both_low = halves(both)
            rows = pl.ds((l * PATCH_DEV + p) * OFFSETS * PATCH, OFFSETS * PATCH)
            first = dot(jnp.concatenate([both_high, both_low], axis=0), kern_high[rows, :])
            total = first[: 2 * fields] + first[2 * fields :] + dot(both_high, kern_low[rows, :])
            send3[p, pl.ds(2 * l, fields, stride=16), :] = total[:fields, :PATCH] - total[fields:, PATCH:]
            send3[p, pl.ds(2 * l + 1, fields, stride=16), :] = total[fields:, :PATCH] + total[:fields, PATCH:]
        recv3[p, block(column), :] = send3[p, block(column), :]
        across(2, p)

    def home(p, k):
        source, target, sends, receives = stage(3, p)
        time = shifted(k)
        push({"node": 2 * z + core, "freq": time}, source.at[block(time)], target.at[block(column)], sends, receives)

    for p in range(PATCH_DEV):
        rest(2, p, parts - 1).wait_recv()
        send4[p] = transform(1, recv3[p])
        for k in along:
            home(p, k)

        @pl.when(diagonal)
        def _(p=p):
            recv4[p, block(column), :] = send4[p, block(column), :]

        @pl.when(jnp.logical_not(diagonal))
        def _(p=p):
            home(p, 0)

    for p in range(PATCH_DEV):

        @pl.when(diagonal)
        def _(p=p):
            rest(3, p, parts - 1).wait_recv()

        @pl.when(jnp.logical_not(diagonal))
        def _(p=p):
            rest(3, p, parts).wait_recv()

        for f in range(fields):
            out_ref[p, pl.ds(f, 16, stride=fields), :] = recv4[p, pl.ds(f * 16, 16), :]

    for copy in place_copies + halo_copies:
        copy.wait_send()
    for p in range(PATCH_DEV):
        pending(send1.at[p], relay.at[p], parts - 1, relay_send.at[p], relay_recv.at[p, 0]).wait_send()
        for index in range(3):
            rest(index, p, parts - 1).wait_send()

    @pl.when(diagonal)
    def _():
        for index in range(parts - 1):
            place_copy(index).wait_send()
        for p in range(PATCH_DEV):
            rest(3, p, parts - 1).wait_send()

    @pl.when(jnp.logical_not(diagonal))
    def _():
        for p in range(PATCH_DEV):
            rest(3, p, parts).wait_send()


def body(density, coords, weights, neighbours, counts):
    parts = lax.axis_size("freq")
    node_parts = lax.axis_size("node")
    times, fields, width = density.shape
    steps = times * parts
    assert times == 16 and fields == parts and node_parts == 2 * parts and width == WIDTH
    rows = times * fields
    hbm = pl.BlockSpec(memory_space=pltpu.HBM)
    buffer = pltpu.VMEM((PATCH_DEV, steps, PATCH), jnp.float32)
    pairs = PATCH_DEV * OFFSETS * PATCH
    operands = [
        density.reshape(rows, width),
        jnp.asarray(transform_tables(steps)),
        coords,
        weights.reshape(1, width),
        neighbours,
        counts,
        jnp.asarray(laplace_table(steps)),
    ]
    operands = [pltpu.with_memory_space_constraint(operand, pltpu.HBM) for operand in operands]
    result = pl.pallas_call(
        functools.partial(kernel, parts),
        out_shape=jax.ShapeDtypeStruct((PATCH_DEV, rows, PATCH), jnp.float32),
        in_specs=[hbm] * len(operands),
        out_specs=pl.BlockSpec(memory_space=pltpu.VMEM),
        scratch_shapes=[
            pltpu.VMEM((PATCH_DEV, rows, PATCH), jnp.float32),
            pltpu.VMEM((4 * steps, steps), jnp.bfloat16),
            pltpu.VMEM((3, width), jnp.float32),
            pltpu.VMEM((1, width), jnp.float32),
            pltpu.SMEM((PATCH_DEV, NEAR_MOST), jnp.int32),
            pltpu.SMEM((PATCH_DEV,), jnp.int32),
            pltpu.SMEM((2, steps // 2), jnp.float32),
            buffer,
            buffer,
            buffer,
            buffer,
            pltpu.VMEM((3 * PATCH_DEV, steps, PATCH), jnp.float32),
            buffer,
            buffer,
            buffer,
            buffer,
            pltpu.VMEM((16, PATCH), jnp.float32),
            pltpu.VMEM((3, 16, PATCH), jnp.float32),
            pltpu.VMEM((pairs, PATCH), jnp.float32),
            pltpu.VMEM((pairs, PATCH), jnp.float32),
            pltpu.VMEM((8 * pairs, 2 * PATCH), jnp.bfloat16),
            pltpu.VMEM((8 * pairs, 2 * PATCH), jnp.bfloat16),
            pltpu.SemaphoreType.DMA((8,)),
            pltpu.SemaphoreType.REGULAR,
            pltpu.SemaphoreType.DMA((PATCH_DEV,)),
            pltpu.SemaphoreType.DMA((PATCH_DEV, parts)),
            pltpu.SemaphoreType.DMA((4, PATCH_DEV)),
            pltpu.SemaphoreType.DMA((4, PATCH_DEV)),
            pltpu.SemaphoreType.DMA((parts,)),
            pltpu.SemaphoreType.DMA((2, PATCH_DEV)),
            pltpu.SemaphoreType.DMA((2, PATCH_DEV)),
            pltpu.SemaphoreType.DMA((parts - 1,)),
            pltpu.SemaphoreType.DMA,
            pltpu.SemaphoreType.DMA((2,)),
            pltpu.SemaphoreType.DMA((2,)),
        ],
        compiler_params=pltpu.CompilerParams(
            collective_id=0, has_side_effects=True, vmem_limit_bytes=40_000_000
        ),
    )(*operands)
    return jnp.swapaxes(result.reshape(PATCH_DEV, times, fields, PATCH), 0, 1).swapaxes(1, 2).reshape(times, fields, width)


def solution(mesh):
    placed = (P("freq", None, "node"), P(None, "node"), P("node"), P("node", None), P("node"))
    return jax.shard_map(
        body, mesh=mesh, in_specs=placed, out_specs=P("freq", None, "node"), check_vma=False
    )
```

time: 68.6 us -> 65.1 us (0.949)
  the two profiles are of different devices: /device:TPU:23 before, /device:TPU:8 now
where the time goes in v3:
time: 65.1 us; the launch traced here: 64.9 us
  Pallas kernels  64.2 us (99%)
  local copies, waits for them, and re-layouts  0.73 us (1%)
    pallas_call x1, Pallas kernels, body(): pl.pallas_call(functools.partial(kernel, parts), out_shape=jax.ShapeDtype...  64.2 us

profile of v3, /device:TPU:8, one launch (start us, length us, event | category | flops | bytes accessed | tf_op | source)
XLA Modules:
  0.0 64.9 jit_solution(3696069761049659248)
XLA Ops:
  0.0 64.2 %shard_map.73 = f32[2,256,128]{2,1,0:T(8,128)S(1)} custom-call(f32[256,256]{1,0:T(8,128)} %bitcast.10, bf16[1024,256]{1,0:T(8,128)(2,1)} %constant.4.clone.table_hbm, f32[3,256]{1,0:T(4,128)} %coords_hbm.1, f32[1,256]{1,0:T(1,128)} %bitcast.11, s32[2,4]{1,0:T(2,128)} %near_hbm.1, s32[2]{0:T(128)} %counts_hbm.1, f32[2,128]{1,0:T(2,128)} %constant.5.clone.laplace_hbm), custom_call_target="tpu_custom_call" | custom-call | tf_op jit(solution)/shard_map/pallas_call | solution.py:528
  64.2 0.7 %copy.11 = f32[2,16,2,8,128]{4,3,0,2,1:T(8,128)} copy(f32[2,16,2,8,128]{4,3,2,1,0:T(8,128)S(1)} %bitcast.9) | data formatting | bytes 524288 | tf_op jit(solution)/shard_map/reshape | solution.py:574

commit v4 on v3

--- a/solution.py
+++ b/solution.py
@@ -110,7 +110,6 @@
     relay_recv,
     send_sem,
     recv_sem,
-    share_recv,
     halo_send,
     halo_recv,
     spread_send,
@@ -247,7 +246,7 @@
         places[1] = place_own[...]
 
     for p in range(PATCH_DEV):
-        for other in near_first:
+        for other in far_first:
             push(
                 {"node": 2 * other + core},
                 send1.at[p, block(other)],
@@ -365,7 +364,7 @@
         kern_low[into, PATCH : 2 * PATCH] = imag_low
         return carry
 
-    lax.fori_loop(0, 4 * blocks, generate, 0)
+    lax.fori_loop(0, 6 * blocks, generate, 0)
 
     def transform(index, data):
         data_high, data_low = halves(data)
@@ -374,17 +373,16 @@
         first = dot(table_high, jnp.concatenate([data_high, data_low], axis=1))
         return first[:, :PATCH] + first[:, PATCH:] + dot(table_low, data_high)
 
-    def across(index, p, receives=None):
-        source, target, sends, arrivals = stage(index, p)
-        receives = arrivals if receives is None else receives
+    def across(index, p):
+        source, target, sends, receives = stage(index, p)
         for other in far_first:
             push({"node": 2 * other + core}, source.at[block(other)], target.at[block(column)], sends, receives)
 
-    def forward_transform(p, receives=None):
+    def forward_transform(p):
         rest(0, p, parts - 1).wait_recv()
         send2[p] = transform(0, recv1[p])
         halo[2 + p, block(column), :] = send2[p, block(column), :]
-        across(1, p, receives)
+        across(1, p)
 
     sides = ((right, 0), (left, 4))
 
@@ -400,35 +398,14 @@
 
     halo_copies = [halo_copy(p, slot, device) for p in range(PATCH_DEV) for device, slot in sides]
 
-    def share_chunk(p, index):
-        for device, slot in sides:
-            push(
-                device,
-                halo.at[2 + p, block(index)],
-                halo.at[slot + p, block(index)],
-                halo_send.at[slot // 4, p],
-                halo_recv.at[slot // 4, p],
-            )
-
     loads[7].wait()
-    forward_transform(0)
-    forward_transform(1, share_recv.at[column])
-    share_chunk(1, column)
-    lax.fori_loop(4 * blocks, 6 * blocks, generate, 0)
-    rest(1, 0, parts - 1).wait_recv()
-    for copy in halo_copies[:2]:
-        copy.start()
-    for other in near_first:
-        pltpu.make_async_remote_copy(
-            src_ref=halo.at[3, block(other)],
-            dst_ref=halo.at[3, block(other)],
-            send_sem=send_sem.at[1, 1],
-            recv_sem=share_recv.at[other],
-            device_id=right,
-            device_id_type=MESH,
-        ).wait_recv()
-        share_chunk(1, other)
+    for p in range(PATCH_DEV):
+        forward_transform(p)
     lax.fori_loop(6 * blocks, 8 * blocks, generate, 0)
+    for p in range(PATCH_DEV):
+        rest(1, p, parts - 1).wait_recv()
+        for copy in halo_copies[2 * p : 2 * p + 2]:
+            copy.start()
     for copy in halo_copies:
         copy.wait_recv()
 
@@ -559,7 +536,6 @@
             pltpu.SemaphoreType.DMA((PATCH_DEV, parts)),
             pltpu.SemaphoreType.DMA((4, PATCH_DEV)),
             pltpu.SemaphoreType.DMA((4, PATCH_DEV)),
-            pltpu.SemaphoreType.DMA((parts,)),
             pltpu.SemaphoreType.DMA((2, PATCH_DEV)),
             pltpu.SemaphoreType.DMA((2, PATCH_DEV)),
             pltpu.SemaphoreType.DMA((parts - 1,)),

time: 65.1 us -> 64.9 us (level)
  no operation moved by 1% of the time
where the time goes in v4:
time: 64.9 us; the launch traced here: 64.8 us
  Pallas kernels  64 us (99%)
  local copies, waits for them, and re-layouts  0.73 us (1%)
    pallas_call x1, Pallas kernels, body(): pl.pallas_call(functools.partial(kernel, parts), out_shape=jax.ShapeDtype...  64 us

profile of v4, /device:TPU:8, one launch (start us, length us, event | category | flops | bytes accessed | tf_op | source)
XLA Modules:
  0.0 64.8 jit_solution(6160180458218708936)
XLA Ops:
  0.0 64.0 %shard_map.73 = f32[2,256,128]{2,1,0:T(8,128)S(1)} custom-call(f32[256,256]{1,0:T(8,128)} %bitcast.10, bf16[1024,256]{1,0:T(8,128)(2,1)} %constant.4.clone.table_hbm, f32[3,256]{1,0:T(4,128)} %coords_hbm.1, f32[1,256]{1,0:T(1,128)} %bitcast.11, s32[2,4]{1,0:T(2,128)} %near_hbm.1, s32[2]{0:T(128)} %counts_hbm.1, f32[2,128]{1,0:T(2,128)} %constant.5.clone.laplace_hbm), custom_call_target="tpu_custom_call" | custom-call | tf_op jit(solution)/shard_map/pallas_call | solution.py:505
  64.0 0.7 %copy.11 = f32[2,16,2,8,128]{4,3,0,2,1:T(8,128)} copy(f32[2,16,2,8,128]{4,3,2,1,0:T(8,128)S(1)} %bitcast.9) | data formatting | bytes 524288 | tf_op jit(solution)/shard_map/reshape | solution.py:550
